TPU v7x, 32 devices: a whole 2x2x4 slice. The times are simulated.
32 devices in a mesh: node: 16 (over z, y, x), hand: 2 (over core).
Axes of the slice: x: 2, y: 2, z: 4, core: 2. Of those that a mesh axis runs over, the one named last changes fastest.
Arguments:
- ranges: bfloat16 [512, 128, 1326], P('node', None, 'hand'), may hold values from 0.00019931793 to 0.0039978027
- strengths: int32 [512, 1326], P('node'), may hold values from 0 to 399
- live_hands: int32 [512, 1326], P('node'), may hold values 0 or 1
- pot_sizes: float32 [512, 128], P('node'), may hold values from 1 to 16
- action_counts: int32 [512], P('node'), may hold values from 1 to 8
- parents: int32 [512], P('node'), may hold values from 0 to 63
- turn_counts: int32 [16], replicated, may hold values from 1 to 4
- root_reach: float32 [16, 2, 1326], P(None, None, 'hand'), may hold values from 0.01 to 1
Outputs:
- turn_values: float32 [16, 2, 1326], P('node', None, 'hand')
- exploitability: float32 [], replicated
All inputs are finite; a program needn't handle non-finite values. No bound on the sum of `live_hands` on one device may be relied on, other than what follows from the above.
Results may differ from a plain program's by a relative error of at most 0.0003.
Values may be sent and summed in bfloat16 or wider, within the bound.
A program may use at most 128 MiB of HBM per device.

v0:
```python
import functools

import jax
import jax.numpy as jnp
import numpy as np
from jax import lax
from jax.experimental import pallas as pl
from jax.experimental.pallas import tpu as pltpu
from jax.sharding import PartitionSpec as P

ACT = 8
GROUPS = 8
TACT = 4
LANE = 128
MESH = pl.DeviceIdType.MESH
GROUP = 4
MID = 200.0
LOW = -1e30


def card_rows(hands, half, padded):
    pairs = [(a, b) for a in range(52) for b in range(a + 1, 52)][:hands]
    flat = np.array(pairs, np.float32).T
    rows = np.zeros((2, 8, padded), np.float32)
    for part in range(2):
        rows[part, :2, :half] = flat[:, part * half : (part + 1) * half]
    return jnp.asarray(rows)


def kernel(
    sizes,
    ranges,
    strengths,
    live,
    pots,
    legal,
    parents,
    turn_legal,
    reach,
    cards,
    best_out,
    total_out,
    held,
    row_s,
    row_live,
    col_s,
    col_pot,
    compat,
    signs,
    tall_s,
    wide_s,
    lines,
    river,
    part,
    got,
    shares,
    local_sem,
    send_sem,
    recv_sem,
    out_sem,
    in_sem,
    tell_sem,
    told_sem,
):
    n_node, nodes, half, padded, turns_mine, rows_all = sizes
    f32, bf16 = jnp.float32, jnp.bfloat16
    node = lax.axis_index("node")
    hand = lax.axis_index("hand")
    me = node * 2 + hand
    n_dev = 2 * n_node
    line_cols = lines.shape[1]
    steps = nodes // GROUP

    barrier = pltpu.get_barrier_semaphore()

    def greet(offset, carry):
        other = lax.rem(me + offset, n_dev)
        pl.semaphore_signal(
            barrier,
            inc=1,
            device_id=(other // 2, lax.rem(other, 2)),
            device_id_type=MESH,
        )
        return carry

    lax.fori_loop(1, n_dev, greet, 0)

    def local_copy(step):
        span = pl.ds(step * GROUP, GROUP)
        return pltpu.make_async_copy(
            ranges.at[span], held.at[hand, span], local_sem.at[step]
        )

    def peer_copy(step):
        span = pl.ds(step * GROUP, GROUP)
        return pltpu.make_async_remote_copy(
            src_ref=ranges.at[span],
            dst_ref=held.at[hand, span],
            send_sem=send_sem.at[step],
            recv_sem=recv_sem.at[step],
            device_id=(node, 1 - hand),
            device_id_type=MESH,
        )

    for step in range(steps):
        local_copy(step).start()

    row_s[...] = jnp.zeros_like(row_s)
    strength = strengths[...].astype(f32) - MID
    alive = live[...].astype(f32)
    for side in range(2):
        cut = slice(side * half, (side + 1) * half)
        row_s[side, :nodes, :half] = strength[:, cut]
        row_s[side, nodes : nodes + 8, :] = cards[side]
        row_live[side, :, :half] = alive[:, cut]
    lines[...] = jnp.zeros_like(lines)

    pl.semaphore_wait(barrier, n_dev - 1)
    for step in range(steps):
        peer_copy(step).start()

    for side in range(2):
        for tile in range(padded // LANE):
            block = row_s[side, :, tile * LANE : (tile + 1) * LANE]
            at = side * padded + tile * LANE
            col_s[at : at + LANE, :] = block.T
    pot_block = jnp.concatenate(
        [pots[...], jnp.zeros((LANE - nodes, line_cols), f32)], axis=0
    )
    col_pot[...] = pot_block.T

    hero_first = row_s[hand, nodes : nodes + 1, :]
    hero_second = row_s[hand, nodes + 1 : nodes + 2, :]

    def compat_rows(tile, carry):
        at = pl.ds(pl.multiple_of(tile * LANE, LANE), LANE)
        first = jnp.broadcast_to(col_s[at, nodes : nodes + 1], (LANE, LANE))
        second = jnp.broadcast_to(col_s[at, nodes + 1 : nodes + 2], (LANE, LANE))
        for column in range(padded // LANE):
            cut = slice(column * LANE, (column + 1) * LANE)
            a = hero_first[:, cut]
            b = hero_second[:, cut]
            shared = (first == a) | (first == b) | (second == a) | (second == b)
            compat[at, cut] = jnp.where(shared, 0.0, 1.0).astype(bf16)
        return carry

    lax.fori_loop(0, 2 * padded // LANE, compat_rows, 0)

    action = lax.broadcasted_iota(jnp.int32, (1, ACT, padded), 1)

    def one_group(step, carry):
        local_copy(step).wait()
        peer_copy(step).wait_recv()
        for first_of in range(0, GROUP, 2):
            pair = (first_of, first_of + 1)
            for u in pair:
                n = step * GROUP + u
                for side in range(2):
                    scaled = held[side, n] * row_live[side, pl.ds(n, 1), :half].astype(bf16)
                    lines[u, :, side * padded : side * padded + half] = scaled
            for u in pair:
                hero = row_s[hand, pl.ds(step * GROUP + u, 1), :]
                tall_s[u] = jnp.broadcast_to(hero, (16, padded)).astype(bf16)
            for tile in range(2 * padded // LANE):
                at = slice(tile * LANE, (tile + 1) * LANE)
                for u in pair:
                    wide = jnp.broadcast_to(col_s[at, u : u + 1], (LANE, 2 * LANE))
                    wide_s[u, at, :] = wide.astype(bf16)
                columns = [wide_s[u, at, :] for u in pair]
                for column in range(padded // (2 * LANE)):
                    cut = slice(column * 2 * LANE, (column + 1) * 2 * LANE)
                    upper = compat[at, cut]
                    lower = -upper
                    for u, column_s in zip(pair, columns):
                        gap = jnp.concatenate([tall_s[u, :, cut]] * (LANE // 16), axis=0) - column_s
                        signs[u, at, cut] = jnp.maximum(jnp.minimum(gap, upper), lower)
            for u in pair:
                n = step * GROUP + u
                values = jnp.dot(lines[u], signs[u], preferred_element_type=f32)
                values = values * col_pot[:, u : u + 1]
                values = values.reshape(2 * GROUPS, ACT, padded)
                values = jnp.where(action < legal[n], values, LOW)
                for shift in (4, 2, 1):
                    values = jnp.maximum(values, pltpu.roll(values, shift, 1))
                for player in range(2):
                    best = values[player * GROUPS]
                    for g in range(1, GROUPS):
                        best = best + values[player * GROUPS + g]
                    best = best[:1] * row_live[hand, pl.ds(n, 1), :]
                    river[player, pl.ds(n, 1), :] = best
        col_s[...] = pltpu.roll(col_s[...], LANE - GROUP, 1)
        col_pot[...] = pltpu.roll(col_pot[...], LANE - GROUP, 1)
        return carry

    row_live[:, :, half:] = jnp.zeros((2, nodes, padded - half), f32)
    lax.fori_loop(0, steps, one_group, 0)

    row_at = lax.broadcasted_iota(jnp.int32, (rows_all, nodes), 0)
    wanted = (row_at // (2 * TACT)) * TACT + lax.rem(row_at, TACT)
    match = parents[...] == wanted
    sums = jnp.zeros((rows_all, padded), f32)
    for player in range(2):
        mine = lax.rem(row_at // TACT, 2) == player
        chosen = jnp.where(match & mine, 1.0, 0.0).astype(bf16)
        rest = river[player]
        for _ in range(3):
            piece = rest.astype(bf16)
            sums = sums + jnp.dot(chosen, piece, preferred_element_type=f32)
            rest = rest - piece.astype(f32)
    block_rows = turns_mine * 2 * TACT
    part[...] = sums.reshape(n_node, block_rows, padded)

    def deal(offset):
        other = lax.rem(node + offset, n_node)
        return pltpu.make_async_remote_copy(
            src_ref=part.at[other],
            dst_ref=got.at[offset - 1],
            send_sem=out_sem.at[offset - 1],
            recv_sem=in_sem.at[offset - 1],
            device_id=(other, hand),
            device_id_type=MESH,
        )

    def deal_start(offset, carry):
        deal(offset).start()
        return carry

    lax.fori_loop(1, n_node, deal_start, 0)

    def add_in(offset, total):
        deal(offset).wait_recv()
        return total + got[offset - 1]

    total = lax.fori_loop(1, n_node, add_in, part[node])

    kind = lax.rem(lax.broadcasted_iota(jnp.int32, (2 * TACT, padded), 0), TACT)
    share = jnp.zeros((1, half), f32)
    for t in range(turns_mine):
        turn = node * turns_mine + t
        mine = total[t * 2 * TACT : (t + 1) * 2 * TACT]
        mine = jnp.where(kind < turn_legal[turn], mine, LOW)
        for player in range(2):
            best = jnp.max(mine[player * TACT : (player + 1) * TACT], axis=0, keepdims=True)
            best = best[:, :half]
            best_out[t, player : player + 1, :] = best
            share = share + reach[turn, player : player + 1, :] * best
    shares[me] = jnp.broadcast_to(jnp.sum(share, axis=1, keepdims=True), (8, LANE))

    def tell(offset, back):
        other = lax.rem(me + offset, n_dev)
        source = lax.rem(me + n_dev - offset, n_dev) if back else me
        return pltpu.make_async_remote_copy(
            src_ref=shares.at[me],
            dst_ref=shares.at[source],
            send_sem=tell_sem.at[offset - 1],
            recv_sem=told_sem.at[offset - 1],
            device_id=(other // 2, lax.rem(other, 2)),
            device_id_type=MESH,
        )

    def tell_start(offset, carry):
        tell(offset, False).start()
        return carry

    def tell_wait(offset, carry):
        tell(offset, True).wait_recv()
        return carry

    lax.fori_loop(1, n_dev, tell_start, 0)
    lax.fori_loop(1, n_dev, tell_wait, 0)
    whole = jnp.zeros((8, LANE), f32)
    for device in range(n_dev):
        whole = whole + shares[device]
    total_out[0, 0] = whole[0, 0]

    for step in range(steps):
        peer_copy(step).wait_send()

    def done(offset, carry):
        deal(offset).wait_send()
        return carry

    def done_tell(offset, carry):
        tell(offset, False).wait_send()
        return carry

    lax.fori_loop(1, n_node, done, 0)
    lax.fori_loop(1, n_dev, done_tell, 0)


def solution(mesh):
    n_node = mesh.shape["node"]

    def local(
        ranges, strengths, live_hands, pot_sizes, action_counts, parents, turn_counts, root_reach
    ):
        nodes, line_cols, half = ranges.shape
        hands = strengths.shape[1]
        padded = -(-half // 256) * 256
        turns_all = turn_counts.shape[0]
        turns_mine = turns_all // n_node
        rows_all = turns_all * 2 * TACT
        steps = nodes // GROUP
        f32, bf16 = jnp.float32, jnp.bfloat16
        vmem = pl.BlockSpec(memory_space=pltpu.VMEM)
        smem = pl.BlockSpec(memory_space=pltpu.SMEM)
        hbm = pl.BlockSpec(memory_space=pl.ANY)
        dma = pltpu.SemaphoreType.DMA
        best, total = pl.pallas_call(
            functools.partial(kernel, (n_node, nodes, half, padded, turns_mine, rows_all)),
            out_shape=(
                jax.ShapeDtypeStruct((turns_mine, 2, half), f32),
                jax.ShapeDtypeStruct((1, 1), f32),
            ),
            in_specs=[hbm, vmem, vmem, vmem, smem, vmem, smem, vmem, vmem],
            out_specs=(vmem, smem),
            scratch_shapes=[
                pltpu.VMEM((2, nodes, line_cols, half), bf16),
                pltpu.VMEM((2, LANE, padded), f32),
                pltpu.VMEM((2, nodes, padded), f32),
                pltpu.VMEM((2 * padded, LANE), f32),
                pltpu.VMEM((line_cols, LANE), f32),
                pltpu.VMEM((2 * padded, padded), bf16),
                pltpu.VMEM((GROUP, 2 * padded, padded), bf16),
                pltpu.VMEM((GROUP, 16, padded), bf16),
                pltpu.VMEM((GROUP, 2 * padded, 2 * LANE), bf16),
                pltpu.VMEM((GROUP, line_cols, 2 * padded), bf16),
                pltpu.VMEM((2, nodes, padded), f32),
                pltpu.VMEM((n_node, turns_mine * 2 * TACT, padded), f32),
                pltpu.VMEM((n_node - 1, turns_mine * 2 * TACT, padded), f32),
                pltpu.VMEM((2 * n_node, 8, LANE), f32),
                dma((steps,)),
                dma((steps,)),
                dma((steps,)),
                dma((n_node - 1,)),
                dma((n_node - 1,)),
                dma((2 * n_node - 1,)),
                dma((2 * n_node - 1,)),
            ],
            compiler_params=pltpu.CompilerParams(
                collective_id=0, has_side_effects=True, vmem_limit_bytes=60 * 1024 * 1024
            ),
        )(
            ranges,
            strengths,
            live_hands,
            pot_sizes,
            action_counts,
            parents.reshape(1, nodes),
            turn_counts,
            root_reach,
            card_rows(hands, half, padded),
        )
        return best, total.reshape(())

    in_specs = (
        P("node", None, "hand"),
        P("node", None),
        P("node", None),
        P("node", None),
        P("node"),
        P("node"),
        P(),
        P(None, None, "hand"),
    )
    out_specs = (P("node", None, "hand"), P())
    return jax.shard_map(local, mesh=mesh, in_specs=in_specs, out_specs=out_specs, check_vma=False)
```

profile of v0, /device:TPU:0, one launch (start us, length us, event | category | flops | bytes accessed | tf_op | source)
XLA Modules:
  0.0 69.0 jit_solution(6525109542600104467)
XLA Ops:
  0.6 9.2 %copy.11.ranges = bf16[32,128,663]{2,1,0:T(8,128)(2,1)} copy(bf16[32,128,663]{1,0,2:T(8,128)(2,1)} %param.9) | data formatting | bytes 10862592 | tf_op args[0]
  9.8 56.1 %shard_map.104 = (f32[1,2,663]{2,1,0:T(2,128)}, f32[1,1]{1,0:T(1,128)}) custom-call(bf16[32,128,663]{2,1,0:T(8,128)(2,1)} %copy.11.ranges, s32[32,1326]{1,0:T(8,128)} %strengths.1, s32[32,1326]{1,0:T(8,128)} %live.1, f32[32,128]{1,0:T(8,128)} %pots.1, s32[32]{0:T(128)} %legal.1, s32[1,32]{1,0:T(1,128)} %bitcast.2, s32[16]{0:T(128)} %turn_legal.1, ...), custom_call_target="tpu_custom_call" | custom-call | tf_op jit(solution)/shard_map/pallas_call | solution.py:309
  65.9 1.3 %copy.14 = f32[1,2,663]{2,1,0:T(2,128)} copy(f32[1,2,663]{2,1,0:T(2,128)} %get-tuple-element.8) | data formatting | bytes 10608
where the time goes:
time: 69.3 us; the launch traced here: 69 us
  Pallas kernels  56.1 us (81%)
  local copies, waits for them, and re-layouts  10.5 us (15%)
  between operations  2.4 us (3%)
    pallas_call x1, Pallas kernels, local(): pl.pallas_call(functools.partial(kernel, (n_node, nodes, half, padded, tu...  56.1 us
    unnamed x2, local copies, waits for them, and re-layouts  10.5 us

commit v1 on v0

v1 whole, which is shorter than its diff:
```python
import functools

import jax
import jax.numpy as jnp
import numpy as np
from jax import lax
from jax.experimental import pallas as pl
from jax.experimental.pallas import tpu as pltpu
from jax.sharding import PartitionSpec as P

ACT = 8
GROUPS = 8
TACT = 4
LANE = 128
PACK = 16
WIDE = 256
TALL = 8
PAIR = 4
MESH = pl.DeviceIdType.MESH
MID = 200.0
LOW = -1e30


def card_rows(hands, half, tiles):
    pairs = [(a, b) for a in range(52) for b in range(a + 1, 52)][:hands]
    flat = np.array(pairs, np.float32).T
    rows = np.zeros((2, 8, tiles * LANE), np.float32)
    for side in range(2):
        rows[side, :2, :half] = flat[:, side * half : (side + 1) * half]
    return jnp.asarray(rows.reshape(2, 8, tiles, LANE).transpose(0, 2, 1, 3))


def kernel(
    sizes,
    ranges,
    strengths,
    live,
    pots,
    legal,
    parents,
    turn_legal,
    reach,
    cards,
    best_out,
    total_out,
    raw,
    loose,
    lines,
    row_s,
    row_live,
    col_s,
    wide,
    compat,
    pot_wide,
    values,
    river,
    river_in,
    chosen,
    part,
    got_plane,
    mid,
    got_line,
    shares,
    line_shares,
    local_sem,
    send_sem,
    recv_sem,
    river_send,
    river_recv,
    plane_send,
    plane_recv,
    line_send,
    line_recv,
    tell_send,
    tell_recv,
    tell2_send,
    tell2_recv,
):
    n_node, low, high, nodes, half, tiles, turns_mine, rows_all = sizes
    f32, bf16 = jnp.float32, jnp.bfloat16
    node = lax.axis_index("node")
    hand = lax.axis_index("hand")
    q = lax.rem(node, low)
    z = node // low
    mine = nodes // 2
    spans = mine // TALL
    blocks = tiles // 2
    rows_k = tiles * LANE
    used = -(-half // PACK) * PACK
    first_row = pl.multiple_of(hand * mine, TALL)
    line_rows = 2 * GROUPS * ACT
    out_rows = turns_mine * 2 * TACT

    barrier = pltpu.get_barrier_semaphore()

    def plane_device(offset):
        spot = lax.rem(q * 2 + hand + offset, 2 * low)
        return spot, (z * low + spot // 2, lax.rem(spot, 2))

    def line_device(offset):
        spot = lax.rem(z + offset, high)
        return spot, (spot * low + q, hand)

    for offset in range(1, 2 * low):
        pl.semaphore_signal(
            barrier, inc=1, device_id=plane_device(offset)[1], device_id_type=MESH
        )
    for offset in range(1, high):
        pl.semaphore_signal(
            barrier, inc=1, device_id=line_device(offset)[1], device_id_type=MESH
        )

    def local_copy(span):
        at = pl.multiple_of(hand * mine + span * TALL, TALL)
        return pltpu.make_async_copy(
            ranges.at[:, pl.ds(at, TALL), :],
            raw.at[hand, span, pl.ds(0, half)],
            local_sem.at[span],
        )

    def peer_copy(span):
        at = pl.multiple_of((1 - hand) * mine + span * TALL, TALL)
        return pltpu.make_async_remote_copy(
            src_ref=ranges.at[:, pl.ds(at, TALL), :],
            dst_ref=raw.at[hand, span, pl.ds(0, half)],
            send_sem=send_sem.at[span],
            recv_sem=recv_sem.at[span],
            device_id=(node, 1 - hand),
            device_id_type=MESH,
        )

    for span in range(spans):
        local_copy(span).start()

    for side in range(2):
        for span in range(spans):
            raw[side, span, half:] = jnp.zeros((rows_k - half, TALL, LANE), bf16)

    row_s[...] = jnp.zeros_like(row_s)
    row_live[...] = jnp.zeros_like(row_live)
    strength = strengths[pl.ds(first_row, mine), :].astype(f32) - MID
    alive = live[pl.ds(first_row, mine), :].astype(f32)
    for side in range(2):
        for tile in range(tiles):
            width = min(LANE, half - tile * LANE)
            cut = slice(side * half + tile * LANE, side * half + tile * LANE + width)
            row_s[side, tile, :mine, :width] = strength[:, cut]
            row_live[side, tile, :, :width] = alive[:, cut]
            row_s[side, tile, mine : mine + 8, :] = cards[side, tile]

    pl.semaphore_wait(barrier, 2 * low - 1 + high - 1)
    for span in range(spans):
        peer_copy(span).start()

    def turn_rows(tile, carry):
        for side in range(2):
            col_s[side * tiles + tile] = row_s[side, tile].T
        return carry

    lax.fori_loop(0, tiles, turn_rows, 0)

    def compat_rows(tile, carry):
        column = col_s[tile]
        at = pl.ds(pl.multiple_of(tile * LANE, LANE), LANE)
        first = jnp.broadcast_to(column[:, mine : mine + 1], (LANE, LANE)).astype(bf16)
        second = jnp.broadcast_to(column[:, mine + 1 : mine + 2], (LANE, LANE)).astype(bf16)
        one = jnp.ones((LANE, LANE), bf16)
        zero = jnp.zeros((LANE, LANE), bf16)
        for side in range(2):
            for spot in range(tiles):
                a = jnp.broadcast_to(row_s[side, spot, mine : mine + 1, :], (LANE, LANE)).astype(bf16)
                b = jnp.broadcast_to(row_s[side, spot, mine + 1 : mine + 2, :], (LANE, LANE)).astype(bf16)
                shared = (first == a) | (first == b) | (second == a) | (second == b)
                compat[side * tiles + spot, at, :] = jnp.where(shared, zero, one)
        for n in range(mine):
            spread = jnp.broadcast_to(column[:, n : n + 1], (LANE, LANE))
            wide[n, at, :] = spread.astype(bf16)
        return carry

    lax.fori_loop(0, 2 * tiles, compat_rows, 0)

    pot_block = jnp.concatenate(
        [pots[pl.ds(first_row, mine), :], jnp.zeros((LANE - mine, line_rows), f32)], axis=0
    ).T
    for n in range(mine):
        pot_wide[n] = jnp.broadcast_to(pot_block[:, n : n + 1], (line_rows, LANE))

    group = 2 * mine
    depth = 2 * 3 * group
    source = lax.broadcasted_iota(jnp.int32, (group, depth), 0)
    column_at = lax.broadcasted_iota(jnp.int32, (group, depth), 1)
    owner = lax.rem(lax.rem(column_at, group) + hand * mine, group)
    pick = jnp.where(source == owner, 1.0, 0.0).astype(bf16)
    parent_rows = jnp.broadcast_to(parents[...].astype(f32), (16, nodes)).astype(bf16)
    parent_of = jnp.dot(parent_rows, pick, preferred_element_type=f32)[:1]
    row_at = lax.broadcasted_iota(jnp.int32, (rows_all, depth), 0)
    depth_at = lax.broadcasted_iota(jnp.int32, (rows_all, depth), 1)
    wanted = (row_at // (2 * TACT)) * TACT + lax.rem(row_at, TACT)
    same = lax.rem(row_at // TACT, 2) == depth_at // (3 * group)
    match = jnp.broadcast_to(parent_of, (rows_all, depth)) == wanted.astype(f32)
    chosen[...] = jnp.where(match & same, 1.0, 0.0).astype(bf16)

    def spread_lines(side, span):
        def one_tile(tile, carry):
            at = pl.ds(pl.multiple_of(tile * LANE, LANE), LANE)
            loose[...] = raw[side, span, at].astype(f32).reshape(LANE * TALL, LANE)
            for u in range(TALL):
                n = span * TALL + u
                block = loose[pl.ds(u, LANE, stride=TALL), :].astype(bf16).T
                keep = row_live[side, tile, pl.ds(n, 1), :].astype(bf16)
                lines[n, side * tiles + tile] = block * keep
            return carry

        lax.fori_loop(0, tiles, one_tile, 0)

    for span in range(spans):
        local_copy(span).wait()
        spread_lines(hand, span)

    def river_copy(b):
        return pltpu.make_async_remote_copy(
            src_ref=river.at[1 - hand, b],
            dst_ref=river_in.at[b],
            send_sem=river_send.at[b],
            recv_sem=river_recv.at[b],
            device_id=(node, 1 - hand),
            device_id_type=MESH,
        )

    def plane_copy(b, offset):
        spot = lax.rem(q + offset, low)
        return pltpu.make_async_remote_copy(
            src_ref=part.at[b, spot],
            dst_ref=got_plane.at[b, offset - 1],
            send_sem=plane_send.at[b, offset - 1],
            recv_sem=plane_recv.at[b, offset - 1],
            device_id=(z * low + spot, hand),
            device_id_type=MESH,
        )

    def line_copy(b, offset):
        spot, device = line_device(offset)
        return pltpu.make_async_remote_copy(
            src_ref=mid.at[b, spot],
            dst_ref=got_line.at[b, offset - 1],
            send_sem=line_send.at[b, offset - 1],
            recv_sem=line_recv.at[b, offset - 1],
            device_id=device,
            device_id_type=MESH,
        )

    def sum_block(b):
        river_copy(b).wait_recv()
        pieces = []
        for player in range(2):
            rest = jnp.concatenate(
                [
                    jnp.concatenate([river[hand, b, player, j], river_in[b, player, j]], axis=0)
                    for j in range(2)
                ],
                axis=1,
            )
            for _ in range(3):
                piece = rest.astype(bf16)
                pieces.append(piece)
                rest = rest - piece.astype(f32)
        sums = jnp.dot(
            chosen[...], jnp.concatenate(pieces, axis=0), preferred_element_type=f32
        )
        for other in range(n_node):
            part[b, other % low, other // low] = sums[other * out_rows : (other + 1) * out_rows]
        for offset in range(1, low):
            plane_copy(b, offset).start()

    def pass_block(b):
        whole = part[b, q]
        for offset in range(1, low):
            plane_copy(b, offset).wait_recv()
            whole = whole + got_plane[b, offset - 1]
        mid[b] = whole
        for offset in range(1, high):
            line_copy(b, offset).start()

    steps = mine // PAIR

    def one_step(step, carry):
        b = step // steps
        p = lax.rem(step, steps)
        for span in range(spans):

            @pl.when(step == span * TALL // PAIR)
            def _():
                peer_copy(span).wait_recv()
                spread_lines(1 - hand, span)

        for u in range(PAIR):
            n = p * PAIR + u
            left = jnp.concatenate([lines[n, k] for k in range(2 * tiles)], axis=1)
            columns = []
            for side in range(2):
                for j in range(2):
                    hero = row_s[side, 2 * b + j, pl.ds(n, 1), :]
                    hero = jnp.broadcast_to(hero, (PACK, LANE)).astype(bf16)
                    hero = jnp.concatenate([hero] * (used // PACK), axis=0)
                    stack = []
                    for other in range(2):
                        at = slice(other * rows_k, other * rows_k + used)
                        upper = compat[side * tiles + 2 * b + j, at, :]
                        gap = hero - wide[n, at, :]
                        stack.append(lax.clamp(jnp.bfloat16(-1), gap * upper, jnp.bfloat16(1)))
                        if rows_k > used:
                            stack.append(jnp.zeros((rows_k - used, LANE), bf16))
                    columns.append(jnp.concatenate(stack, axis=0))
            signs = jnp.concatenate(columns, axis=1)
            result = jnp.dot(left, signs, preferred_element_type=f32)
            last = jnp.maximum(legal[hand * mine + n] - 1, 0)
            for side in range(2):
                for j in range(2):
                    spot = side * 2 + j
                    values[u, spot] = result[:, spot * LANE : (spot + 1) * LANE] * pot_wide[n]
                    best = values[u, spot, pl.ds(0, 2 * GROUPS, stride=ACT), :]
                    for a in range(1, ACT):
                        row = jnp.minimum(last, a)
                        best = jnp.maximum(
                            best, values[u, spot, pl.ds(row, 2 * GROUPS, stride=ACT), :]
                        )
                    keep = row_live[side, 2 * b + j, pl.ds(n, 1), :]
                    for player in range(2):
                        total = jnp.sum(
                            best[player * GROUPS : (player + 1) * GROUPS], axis=0, keepdims=True
                        )
                        river[side, b, player, j, pl.ds(n, 1), :] = total * keep

        @pl.when(p == steps - 1)
        def _():
            river_copy(b).start()

        @pl.when((p == 0) & (b > 0))
        def _():
            sum_block(b - 1)

        @pl.when((p == steps // 2) & (b > 0))
        def _():
            pass_block(b - 1)

        return carry

    lax.fori_loop(0, blocks * steps, one_step, 0)
    sum_block(blocks - 1)
    pass_block(blocks - 1)

    columns = []
    for b in range(blocks):
        whole = mid[b, z]
        for offset in range(1, high):
            line_copy(b, offset).wait_recv()
            whole = whole + got_line[b, offset - 1]
        columns.append(whole)
    total = jnp.concatenate(columns, axis=1)

    kind = lax.rem(lax.broadcasted_iota(jnp.int32, (2 * TACT, rows_k), 0), TACT)
    share = jnp.zeros((1, half), f32)
    for t in range(turns_mine):
        turn = node * turns_mine + t
        rows = total[t * 2 * TACT : (t + 1) * 2 * TACT]
        rows = jnp.where(kind < turn_legal[turn], rows, LOW)
        for player in range(2):
            best = jnp.max(rows[player * TACT : (player + 1) * TACT], axis=0, keepdims=True)
            best = best[:, :half]
            best_out[t, player : player + 1, :] = best
            share = share + reach[turn, player : player + 1, :] * best
    me = q * 2 + hand
    shares[me] = jnp.broadcast_to(jnp.sum(share, axis=1, keepdims=True), (8, LANE))

    def tell_plane(offset, back):
        to, device = plane_device(offset)
        source = lax.rem(me + 2 * low - offset, 2 * low) if back else me
        return pltpu.make_async_remote_copy(
            src_ref=shares.at[me],
            dst_ref=shares.at[source],
            send_sem=tell_send.at[offset - 1],
            recv_sem=tell_recv.at[offset - 1],
            device_id=device,
            device_id_type=MESH,
        )

    def tell_line(offset, back):
        to, device = line_device(offset)
        source = lax.rem(z + high - offset, high) if back else z
        return pltpu.make_async_remote_copy(
            src_ref=line_shares.at[z],
            dst_ref=line_shares.at[source],
            send_sem=tell2_send.at[offset - 1],
            recv_sem=tell2_recv.at[offset - 1],
            device_id=device,
            device_id_type=MESH,
        )

    for offset in range(1, 2 * low):
        tell_plane(offset, False).start()
    for offset in range(1, 2 * low):
        tell_plane(offset, True).wait_recv()
    whole = shares[0]
    for spot in range(1, 2 * low):
        whole = whole + shares[spot]
    line_shares[z] = whole
    for offset in range(1, high):
        tell_line(offset, False).start()
    for offset in range(1, high):
        tell_line(offset, True).wait_recv()
    whole = line_shares[0]
    for spot in range(1, high):
        whole = whole + line_shares[spot]
    total_out[0, 0] = whole[0, 0]

    for span in range(spans):
        peer_copy(span).wait_send()
    for b in range(blocks):
        river_copy(b).wait_send()
        for offset in range(1, low):
            plane_copy(b, offset).wait_send()
        for offset in range(1, high):
            line_copy(b, offset).wait_send()
    for offset in range(1, 2 * low):
        tell_plane(offset, False).wait_send()
    for offset in range(1, high):
        tell_line(offset, False).wait_send()


def solution(mesh):
    n_node = mesh.shape["node"]
    high = min(4, n_node)
    low = n_node // high

    def local(
        ranges, strengths, live_hands, pot_sizes, action_counts, parents, turn_counts, root_reach
    ):
        nodes, line_rows, half = ranges.shape
        hands = strengths.shape[1]
        tiles = -(-half // WIDE) * 2
        blocks = tiles // 2
        turns_all = turn_counts.shape[0]
        turns_mine = turns_all // n_node
        rows_all = turns_all * 2 * TACT
        out_rows = turns_mine * 2 * TACT
        mine = nodes // 2
        spans = mine // TALL
        f32, bf16 = jnp.float32, jnp.bfloat16
        vmem = pl.BlockSpec(memory_space=pltpu.VMEM)
        smem = pl.BlockSpec(memory_space=pltpu.SMEM)
        hbm = pl.BlockSpec(memory_space=pl.ANY)
        dma = pltpu.SemaphoreType.DMA
        sizes = (n_node, low, high, nodes, half, tiles, turns_mine, rows_all)
        best, total = pl.pallas_call(
            functools.partial(kernel, sizes),
            out_shape=(
                jax.ShapeDtypeStruct((turns_mine, 2, half), f32),
                jax.ShapeDtypeStruct((1, 1), f32),
            ),
            in_specs=[hbm, vmem, vmem, vmem, smem, vmem, smem, vmem, vmem],
            out_specs=(vmem, smem),
            scratch_shapes=[
                pltpu.VMEM((2, spans, tiles * LANE, TALL, line_rows), bf16),
                pltpu.VMEM((LANE * TALL, line_rows), f32),
                pltpu.VMEM((mine, 2 * tiles, line_rows, LANE), bf16),
                pltpu.VMEM((2, tiles, LANE, LANE), f32),
                pltpu.VMEM((2, tiles, mine, LANE), f32),
                pltpu.VMEM((2 * tiles, LANE, LANE), f32),
                pltpu.VMEM((mine, 2 * tiles * LANE, LANE), bf16),
                pltpu.VMEM((2 * tiles, 2 * tiles * LANE, LANE), bf16),
                pltpu.VMEM((mine, line_rows, LANE), f32),
                pltpu.VMEM((PAIR, 4, line_rows, LANE), f32),
                pltpu.VMEM((2, blocks, 2, 2, mine, LANE), f32),
                pltpu.VMEM((blocks, 2, 2, mine, LANE), f32),
                pltpu.VMEM((rows_all, 12 * mine), bf16),
                pltpu.VMEM((blocks, low, high, out_rows, WIDE), f32),
                pltpu.VMEM((blocks, low - 1, high, out_rows, WIDE), f32),
                pltpu.VMEM((blocks, high, out_rows, WIDE), f32),
                pltpu.VMEM((blocks, high - 1, out_rows, WIDE), f32),
                pltpu.VMEM((2 * low, 8, LANE), f32),
                pltpu.VMEM((high, 8, LANE), f32),
                dma((spans,)),
                dma((spans,)),
                dma((spans,)),
                dma((blocks,)),
                dma((blocks,)),
                dma((blocks, low - 1)),
                dma((blocks, low - 1)),
                dma((blocks, high - 1)),
                dma((blocks, high - 1)),
                dma((2 * low - 1,)),
                dma((2 * low - 1,)),
                dma((high - 1,)),
                dma((high - 1,)),
            ],
            compiler_params=pltpu.CompilerParams(
                collective_id=0, has_side_effects=True, vmem_limit_bytes=60 * 1024 * 1024
            ),
        )(
            jnp.transpose(ranges, (2, 0, 1)),
            strengths,
            live_hands,
            pot_sizes,
            action_counts,
            parents.reshape(1, nodes),
            turn_counts,
            root_reach,
            card_rows(hands, half, tiles),
        )
        return best, total.reshape(())

    in_specs = (
        P("node", None, "hand"),
        P("node", None),
        P("node", None),
        P("node", None),
        P("node"),
        P("node"),
        P(),
        P(None, None, "hand"),
    )
    out_specs = (P("node", None, "hand"), P())
    return jax.shard_map(local, mesh=mesh, in_specs=in_specs, out_specs=out_specs, check_vma=False)
```

time: 69.3 us -> 56.6 us (0.82)
  local copies, waits for them, and re-layouts: 10.5 us -> 1.29 us
  Pallas kernels: 56.1 us -> 52.7 us
    unnamed x2 -> x1, local copies, waits for them, and re-layouts: 10.5 us -> 1.29 us
    pallas_call x1, Pallas kernels: 56.1 us -> 52.7 us  [local(): pl.pallas_call(functools.partial(kernel, sizes), out_shape=(jax.ShapeDtyp...]
where the time goes in v1:
time: 56.6 us; the launch traced here: 56.4 us
  Pallas kernels  52.7 us (93%)
  between operations  2.4 us (4%)
  local copies, waits for them, and re-layouts  1.29 us (2%)
    pallas_call x1, Pallas kernels, local(): pl.pallas_call(functools.partial(kernel, sizes), out_shape=(jax.ShapeDtyp...  52.7 us
    unnamed x1, local copies, waits for them, and re-layouts  1.29 us

profile of v1, /device:TPU:0, one launch (start us, length us, event | category | flops | bytes accessed | tf_op | source)
XLA Modules:
  0.0 56.4 jit_solution(18350625629763277888)
XLA Ops:
  0.6 52.7 %shard_map.104 = (f32[1,2,663]{2,1,0:T(2,128)}, f32[1,1]{1,0:T(1,128)}) custom-call(bf16[663,32,128]{2,1,0:T(8,128)(2,1)} %bitcast.3, s32[32,1326]{1,0:T(8,128)} %strengths.1, s32[32,1326]{1,0:T(8,128)} %live.1, f32[32,128]{1,0:T(8,128)} %pots.1, s32[32]{0:T(128)} %legal.1, s32[1,32]{1,0:T(1,128)} %bitcast.4, s32[16]{0:T(128)} %turn_legal.1, ...), custom_call_target="tpu_custom_call" | custom-call | tf_op jit(solution)/shard_map/pallas_call | solution.py:454
  53.3 1.3 %copy.13 = f32[1,2,663]{2,1,0:T(2,128)} copy(f32[1,2,663]{2,1,0:T(2,128)} %get-tuple-element.8) | data formatting | bytes 10608

commit v2 on v1

--- a/solution.py
+++ b/solution.py
@@ -21,13 +21,16 @@
 LOW = -1e30
 
 
-def card_rows(hands, half, tiles):
+def compat_table(hands, half, tiles):
     pairs = [(a, b) for a in range(52) for b in range(a + 1, 52)][:hands]
-    flat = np.array(pairs, np.float32).T
-    rows = np.zeros((2, 8, tiles * LANE), np.float32)
-    for side in range(2):
-        rows[side, :2, :half] = flat[:, side * half : (side + 1) * half]
-    return jnp.asarray(rows.reshape(2, 8, tiles, LANE).transpose(0, 2, 1, 3))
+    holds = np.zeros((hands, 52), np.int32)
+    for hand, (a, b) in enumerate(pairs):
+        holds[hand, a] = holds[hand, b] = 1
+    apart = (holds @ holds.T) == 0
+    table = np.zeros((2, tiles * LANE, 2, tiles * LANE), np.int8)
+    table[:, :half, :, :half] = apart.reshape(2, half, 2, half)
+    table = table.reshape(2 * tiles * LANE, 2 * tiles, LANE).transpose(1, 0, 2)
+    return jnp.asarray(table)
 
 
 def kernel(
@@ -40,7 +43,7 @@
     parents,
     turn_legal,
     reach,
-    cards,
+    table,
     best_out,
     total_out,
     raw,
@@ -50,18 +53,19 @@
     row_live,
     col_s,
     wide,
+    small,
     compat,
     pot_wide,
-    values,
+    turned,
     river,
     river_in,
     chosen,
     part,
     got_plane,
-    mid,
     got_line,
+    found,
     shares,
-    line_shares,
+    table_sem,
     local_sem,
     send_sem,
     recv_sem,
@@ -73,8 +77,6 @@
     line_recv,
     tell_send,
     tell_recv,
-    tell2_send,
-    tell2_recv,
 ):
     n_node, low, high, nodes, half, tiles, turns_mine, rows_all = sizes
     f32, bf16 = jnp.float32, jnp.bfloat16
@@ -88,7 +90,8 @@
     rows_k = tiles * LANE
     used = -(-half // PACK) * PACK
     first_row = pl.multiple_of(hand * mine, TALL)
-    line_rows = 2 * GROUPS * ACT
+    each = 2 * GROUPS
+    line_rows = each * ACT
     out_rows = turns_mine * 2 * TACT
 
     barrier = pltpu.get_barrier_semaphore()
@@ -129,8 +132,10 @@
             device_id_type=MESH,
         )
 
+    table_copy = pltpu.make_async_copy(table, small, table_sem)
     for span in range(spans):
         local_copy(span).start()
+    table_copy.start()
 
     for side in range(2):
         for span in range(spans):
@@ -146,7 +151,6 @@
             cut = slice(side * half + tile * LANE, side * half + tile * LANE + width)
             row_s[side, tile, :mine, :width] = strength[:, cut]
             row_live[side, tile, :, :width] = alive[:, cut]
-            row_s[side, tile, mine : mine + 8, :] = cards[side, tile]
 
     pl.semaphore_wait(barrier, 2 * low - 1 + high - 1)
     for span in range(spans):
@@ -159,21 +163,14 @@
 
     lax.fori_loop(0, tiles, turn_rows, 0)
 
+    table_copy.wait()
+
     def compat_rows(tile, carry):
-        column = col_s[tile]
         at = pl.ds(pl.multiple_of(tile * LANE, LANE), LANE)
-        first = jnp.broadcast_to(column[:, mine : mine + 1], (LANE, LANE)).astype(bf16)
-        second = jnp.broadcast_to(column[:, mine + 1 : mine + 2], (LANE, LANE)).astype(bf16)
-        one = jnp.ones((LANE, LANE), bf16)
-        zero = jnp.zeros((LANE, LANE), bf16)
-        for side in range(2):
-            for spot in range(tiles):
-                a = jnp.broadcast_to(row_s[side, spot, mine : mine + 1, :], (LANE, LANE)).astype(bf16)
-                b = jnp.broadcast_to(row_s[side, spot, mine + 1 : mine + 2, :], (LANE, LANE)).astype(bf16)
-                shared = (first == a) | (first == b) | (second == a) | (second == b)
-                compat[side * tiles + spot, at, :] = jnp.where(shared, zero, one)
+        for spot in range(2 * tiles):
+            compat[spot, at, :] = small[spot, at, :].astype(bf16)
         for n in range(mine):
-            spread = jnp.broadcast_to(column[:, n : n + 1], (LANE, LANE))
+            spread = jnp.broadcast_to(col_s[tile, :, n : n + 1], (LANE, LANE))
             wide[n, at, :] = spread.astype(bf16)
         return carry
 
@@ -182,8 +179,11 @@
     pot_block = jnp.concatenate(
         [pots[pl.ds(first_row, mine), :], jnp.zeros((LANE - mine, line_rows), f32)], axis=0
     ).T
-    for n in range(mine):
-        pot_wide[n] = jnp.broadcast_to(pot_block[:, n : n + 1], (line_rows, LANE))
+    turned[0][...] = pot_block
+    for a in range(ACT):
+        rows = turned[0][pl.ds(a, each, stride=ACT), :]
+        for n in range(mine):
+            pot_wide[n, a * each : (a + 1) * each] = jnp.broadcast_to(rows[:, n : n + 1], (each, LANE))
 
     group = 2 * mine
     depth = 2 * 3 * group
@@ -201,21 +201,31 @@
     chosen[...] = jnp.where(match & same, 1.0, 0.0).astype(bf16)
 
     def spread_lines(side, span):
-        def one_tile(tile, carry):
-            at = pl.ds(pl.multiple_of(tile * LANE, LANE), LANE)
-            loose[...] = raw[side, span, at].astype(f32).reshape(LANE * TALL, LANE)
+        for tile in range(tiles):
+            width = min(LANE, -(-(half - tile * LANE) // PACK) * PACK)
+            bank = tile % 2
+            block = raw[side, span, tile * LANE : tile * LANE + width].astype(f32)
+            loose[bank][: width * TALL] = block.reshape(width * TALL, LANE)
             for u in range(TALL):
                 n = span * TALL + u
-                block = loose[pl.ds(u, LANE, stride=TALL), :].astype(bf16).T
-                keep = row_live[side, tile, pl.ds(n, 1), :].astype(bf16)
-                lines[n, side * tiles + tile] = block * keep
-            return carry
-
-        lax.fori_loop(0, tiles, one_tile, 0)
-
-    for span in range(spans):
+                turn = turned[bank * TALL + u]
+                turn[:, :width] = loose[bank][pl.ds(u, width, stride=TALL), :].T
+                keep = row_live[side, tile, pl.ds(n, 1), :width]
+                for a in range(ACT):
+                    rows = turn[pl.ds(a, each, stride=ACT), :][:, :width] * keep
+                    at = slice(a * each, (a + 1) * each)
+                    lines[n, side * tiles + tile, at, :width] = rows.astype(bf16)
+
+    for n in range(mine):
+        for side in range(2):
+            lines[n, side * tiles + half // LANE] = jnp.zeros((line_rows, LANE), bf16)
+
+    def own_span(span, carry):
         local_copy(span).wait()
         spread_lines(hand, span)
+        return carry
+
+    lax.fori_loop(0, spans, own_span, 0)
 
     def river_copy(b):
         return pltpu.make_async_remote_copy(
@@ -238,11 +248,12 @@
             device_id_type=MESH,
         )
 
-    def line_copy(b, offset):
+    def line_copy(b, offset, back=False):
         spot, device = line_device(offset)
+        source = lax.rem(z + high - offset, high) if back else z
         return pltpu.make_async_remote_copy(
-            src_ref=mid.at[b, spot],
-            dst_ref=got_line.at[b, offset - 1],
+            src_ref=got_line.at[b, z],
+            dst_ref=got_line.at[b, source],
             send_sem=line_send.at[b, offset - 1],
             recv_sem=line_recv.at[b, offset - 1],
             device_id=device,
@@ -277,22 +288,11 @@
         for offset in range(1, low):
             plane_copy(b, offset).wait_recv()
             whole = whole + got_plane[b, offset - 1]
-        mid[b] = whole
+        got_line[b, z] = whole
         for offset in range(1, high):
             line_copy(b, offset).start()
 
-    steps = mine // PAIR
-
-    def one_step(step, carry):
-        b = step // steps
-        p = lax.rem(step, steps)
-        for span in range(spans):
-
-            @pl.when(step == span * TALL // PAIR)
-            def _():
-                peer_copy(span).wait_recv()
-                spread_lines(1 - hand, span)
-
+    def one_step(b, p, carry):
         for u in range(PAIR):
             n = p * PAIR + u
             left = jnp.concatenate([lines[n, k] for k in range(2 * tiles)], axis=1)
@@ -313,17 +313,15 @@
                     columns.append(jnp.concatenate(stack, axis=0))
             signs = jnp.concatenate(columns, axis=1)
             result = jnp.dot(left, signs, preferred_element_type=f32)
-            last = jnp.maximum(legal[hand * mine + n] - 1, 0)
+            count = legal[hand * mine + n]
             for side in range(2):
                 for j in range(2):
                     spot = side * 2 + j
-                    values[u, spot] = result[:, spot * LANE : (spot + 1) * LANE] * pot_wide[n]
-                    best = values[u, spot, pl.ds(0, 2 * GROUPS, stride=ACT), :]
+                    rows = result[:, spot * LANE : (spot + 1) * LANE]
+                    best = rows[:each] * pot_wide[n, :each]
                     for a in range(1, ACT):
-                        row = jnp.minimum(last, a)
-                        best = jnp.maximum(
-                            best, values[u, spot, pl.ds(row, 2 * GROUPS, stride=ACT), :]
-                        )
+                        at = slice(a * each, (a + 1) * each)
+                        best = jnp.maximum(best, jnp.where(a < count, rows[at] * pot_wide[n, at], LOW))
                     keep = row_live[side, 2 * b + j, pl.ds(n, 1), :]
                     for player in range(2):
                         total = jnp.sum(
@@ -331,46 +329,53 @@
                         )
                         river[side, b, player, j, pl.ds(n, 1), :] = total * keep
 
-        @pl.when(p == steps - 1)
-        def _():
-            river_copy(b).start()
-
-        @pl.when((p == 0) & (b > 0))
-        def _():
-            sum_block(b - 1)
-
-        @pl.when((p == steps // 2) & (b > 0))
-        def _():
-            pass_block(b - 1)
-
         return carry
 
-    lax.fori_loop(0, blocks * steps, one_step, 0)
+    steps = TALL // PAIR
+    for b in range(blocks):
+        for span in range(spans):
+            if b == 0:
+                peer_copy(span).wait_recv()
+                spread_lines(1 - hand, span)
+            lax.fori_loop(span * steps, (span + 1) * steps, functools.partial(one_step, b), 0)
+            if b > 0 and span == 0:
+                sum_block(b - 1)
+            if b > 0 and span == spans - 1:
+                pass_block(b - 1)
+        river_copy(b).start()
     sum_block(blocks - 1)
     pass_block(blocks - 1)
 
-    columns = []
     for b in range(blocks):
-        whole = mid[b, z]
         for offset in range(1, high):
-            line_copy(b, offset).wait_recv()
-            whole = whole + got_line[b, offset - 1]
-        columns.append(whole)
-    total = jnp.concatenate(columns, axis=1)
-
-    kind = lax.rem(lax.broadcasted_iota(jnp.int32, (2 * TACT, rows_k), 0), TACT)
-    share = jnp.zeros((1, half), f32)
-    for t in range(turns_mine):
-        turn = node * turns_mine + t
-        rows = total[t * 2 * TACT : (t + 1) * 2 * TACT]
-        rows = jnp.where(kind < turn_legal[turn], rows, LOW)
-        for player in range(2):
-            best = jnp.max(rows[player * TACT : (player + 1) * TACT], axis=0, keepdims=True)
-            best = best[:, :half]
-            best_out[t, player : player + 1, :] = best
-            share = share + reach[turn, player : player + 1, :] * best
+            line_copy(b, offset, True).wait_recv()
+    kind = lax.rem(lax.broadcasted_iota(jnp.int32, (2 * TACT, WIDE), 0), TACT)
+    share = jnp.zeros((1, WIDE), f32)
+    for row in range(high):
+        for t in range(turns_mine):
+            turn = (row * low + q) * turns_mine + t
+            at = slice(t * 2 * TACT, (t + 1) * 2 * TACT)
+            for b in range(blocks):
+                width = min(WIDE, half - b * WIDE)
+                cut = slice(b * WIDE, b * WIDE + width)
+                total = got_line[b, 0, row, at]
+                for other in range(1, high):
+                    total = total + got_line[b, other, row, at]
+                total = jnp.where(kind < turn_legal[turn], total, LOW)
+                for player in range(2):
+                    best = jnp.max(
+                        total[player * TACT : (player + 1) * TACT], axis=0, keepdims=True
+                    )[:, :width]
+                    found[row, t, player : player + 1, cut] = best
+                    part_of = reach[turn, player : player + 1, cut] * best
+                    if width < WIDE:
+                        part_of = jnp.concatenate(
+                            [part_of, jnp.zeros((1, WIDE - width), f32)], axis=1
+                        )
+                    share = share + part_of
+    best_out[...] = found[z]
     me = q * 2 + hand
-    shares[me] = jnp.broadcast_to(jnp.sum(share, axis=1, keepdims=True), (8, LANE))
+    shares[me] = jnp.broadcast_to(jnp.sum(share, axis=1, keepdims=True), (1, LANE))
 
     def tell_plane(offset, back):
         to, device = plane_device(offset)
@@ -384,18 +389,6 @@
             device_id_type=MESH,
         )
 
-    def tell_line(offset, back):
-        to, device = line_device(offset)
-        source = lax.rem(z + high - offset, high) if back else z
-        return pltpu.make_async_remote_copy(
-            src_ref=line_shares.at[z],
-            dst_ref=line_shares.at[source],
-            send_sem=tell2_send.at[offset - 1],
-            recv_sem=tell2_recv.at[offset - 1],
-            device_id=device,
-            device_id_type=MESH,
-        )
-
     for offset in range(1, 2 * low):
         tell_plane(offset, False).start()
     for offset in range(1, 2 * low):
@@ -403,14 +396,6 @@
     whole = shares[0]
     for spot in range(1, 2 * low):
         whole = whole + shares[spot]
-    line_shares[z] = whole
-    for offset in range(1, high):
-        tell_line(offset, False).start()
-    for offset in range(1, high):
-        tell_line(offset, True).wait_recv()
-    whole = line_shares[0]
-    for spot in range(1, high):
-        whole = whole + line_shares[spot]
     total_out[0, 0] = whole[0, 0]
 
     for span in range(spans):
@@ -423,8 +408,6 @@
             line_copy(b, offset).wait_send()
     for offset in range(1, 2 * low):
         tell_plane(offset, False).wait_send()
-    for offset in range(1, high):
-        tell_line(offset, False).wait_send()
 
 
 def solution(mesh):
@@ -457,28 +440,29 @@
                 jax.ShapeDtypeStruct((turns_mine, 2, half), f32),
                 jax.ShapeDtypeStruct((1, 1), f32),
             ),
-            in_specs=[hbm, vmem, vmem, vmem, smem, vmem, smem, vmem, vmem],
+            in_specs=[hbm, vmem, vmem, vmem, smem, vmem, smem, vmem, hbm],
             out_specs=(vmem, smem),
             scratch_shapes=[
                 pltpu.VMEM((2, spans, tiles * LANE, TALL, line_rows), bf16),
-                pltpu.VMEM((LANE * TALL, line_rows), f32),
+                [pltpu.VMEM((LANE * TALL, line_rows), f32) for _ in range(2)],
                 pltpu.VMEM((mine, 2 * tiles, line_rows, LANE), bf16),
                 pltpu.VMEM((2, tiles, LANE, LANE), f32),
                 pltpu.VMEM((2, tiles, mine, LANE), f32),
                 pltpu.VMEM((2 * tiles, LANE, LANE), f32),
                 pltpu.VMEM((mine, 2 * tiles * LANE, LANE), bf16),
+                pltpu.VMEM((2 * tiles, 2 * tiles * LANE, LANE), jnp.int8),
                 pltpu.VMEM((2 * tiles, 2 * tiles * LANE, LANE), bf16),
                 pltpu.VMEM((mine, line_rows, LANE), f32),
-                pltpu.VMEM((PAIR, 4, line_rows, LANE), f32),
+                [pltpu.VMEM((line_rows, LANE), f32) for _ in range(2 * TALL)],
                 pltpu.VMEM((2, blocks, 2, 2, mine, LANE), f32),
                 pltpu.VMEM((blocks, 2, 2, mine, LANE), f32),
                 pltpu.VMEM((rows_all, 12 * mine), bf16),
                 pltpu.VMEM((blocks, low, high, out_rows, WIDE), f32),
                 pltpu.VMEM((blocks, low - 1, high, out_rows, WIDE), f32),
-                pltpu.VMEM((blocks, high, out_rows, WIDE), f32),
-                pltpu.VMEM((blocks, high - 1, out_rows, WIDE), f32),
-                pltpu.VMEM((2 * low, 8, LANE), f32),
-                pltpu.VMEM((high, 8, LANE), f32),
+                pltpu.VMEM((blocks, high, high, out_rows, WIDE), f32),
+                pltpu.VMEM((high, turns_mine, 2, half), f32),
+                pltpu.VMEM((2 * low, 1, LANE), f32),
+                dma,
                 dma((spans,)),
                 dma((spans,)),
                 dma((spans,)),
@@ -490,8 +474,6 @@
                 dma((blocks, high - 1)),
                 dma((2 * low - 1,)),
                 dma((2 * low - 1,)),
-                dma((high - 1,)),
-                dma((high - 1,)),
             ],
             compiler_params=pltpu.CompilerParams(
                 collective_id=0, has_side_effects=True, vmem_limit_bytes=60 * 1024 * 1024
@@ -505,7 +487,7 @@
             parents.reshape(1, nodes),
             turn_counts,
             root_reach,
-            card_rows(hands, half, tiles),
+            compat_table(hands, half, tiles),
         )
         return best, total.reshape(())
 

time: 56.6 us -> 50.7 us (0.90)
  Pallas kernels: 52.7 us -> 46.8 us
    pallas_call x1, Pallas kernels: 52.7 us -> 46.8 us  [local(): pl.pallas_call(functools.partial(kernel, sizes), out_shape=(jax.ShapeDtyp...]
where the time goes in v2:
time: 50.7 us; the launch traced here: 50.5 us
  Pallas kernels  46.8 us (92%)
  between operations  2.4 us (5%)
  local copies, waits for them, and re-layouts  1.29 us (3%)
    pallas_call x1, Pallas kernels, local(): pl.pallas_call(functools.partial(kernel, sizes), out_shape=(jax.ShapeDtyp...  46.8 us
    unnamed x1, local copies, waits for them, and re-layouts  1.29 us

profile of v2, /device:TPU:0, one launch (start us, length us, event | category | flops | bytes accessed | tf_op | source)
XLA Modules:
  0.0 50.5 jit_solution(1476602941275091771)
XLA Ops:
  0.6 46.8 %shard_map.104 = (f32[1,2,663]{2,1,0:T(2,128)}, f32[1,1]{1,0:T(1,128)}) custom-call(bf16[663,32,128]{2,1,0:T(8,128)(2,1)} %bitcast.3, s32[32,1326]{1,0:T(8,128)} %strengths.1, s32[32,1326]{1,0:T(8,128)} %live.1, f32[32,128]{1,0:T(8,128)} %pots.1, s32[32]{0:T(128)} %legal.1, s32[1,32]{1,0:T(1,128)} %bitcast.4, s32[16]{0:T(128)} %turn_legal.1, ...), custom_call_target="tpu_custom_call" | custom-call | tf_op jit(solution)/shard_map/pallas_call | solution.py:437
  47.5 1.3 %copy.13 = f32[1,2,663]{2,1,0:T(2,128)} copy(f32[1,2,663]{2,1,0:T(2,128)} %get-tuple-element.8) | data formatting | bytes 10608

commit v3 on v2

--- a/solution.py
+++ b/solution.py
@@ -54,7 +54,6 @@
     col_s,
     wide,
     small,
-    compat,
     pot_wide,
     turned,
     river,
@@ -167,8 +166,6 @@
 
     def compat_rows(tile, carry):
         at = pl.ds(pl.multiple_of(tile * LANE, LANE), LANE)
-        for spot in range(2 * tiles):
-            compat[spot, at, :] = small[spot, at, :].astype(bf16)
         for n in range(mine):
             spread = jnp.broadcast_to(col_s[tile, :, n : n + 1], (LANE, LANE))
             wide[n, at, :] = spread.astype(bf16)
@@ -305,7 +302,7 @@
                     stack = []
                     for other in range(2):
                         at = slice(other * rows_k, other * rows_k + used)
-                        upper = compat[side * tiles + 2 * b + j, at, :]
+                        upper = small[side * tiles + 2 * b + j, at, :].astype(bf16)
                         gap = hero - wide[n, at, :]
                         stack.append(lax.clamp(jnp.bfloat16(-1), gap * upper, jnp.bfloat16(1)))
                         if rows_k > used:
@@ -451,7 +448,6 @@
                 pltpu.VMEM((2 * tiles, LANE, LANE), f32),
                 pltpu.VMEM((mine, 2 * tiles * LANE, LANE), bf16),
                 pltpu.VMEM((2 * tiles, 2 * tiles * LANE, LANE), jnp.int8),
-                pltpu.VMEM((2 * tiles, 2 * tiles * LANE, LANE), bf16),
                 pltpu.VMEM((mine, line_rows, LANE), f32),
                 [pltpu.VMEM((line_rows, LANE), f32) for _ in range(2 * TALL)],
                 pltpu.VMEM((2, blocks, 2, 2, mine, LANE), f32),

time: 50.7 us -> 48.1 us (0.949)
  Pallas kernels: 46.8 us -> 44.2 us
    pallas_call x1, Pallas kernels: 46.8 us -> 44.2 us  [local(): pl.pallas_call(functools.partial(kernel, sizes), out_shape=(jax.ShapeDtyp...]
where the time goes in v3:
time: 48.1 us; the launch traced here: 47.9 us
  Pallas kernels  44.2 us (92%)
  between operations  2.4 us (5%)
  local copies, waits for them, and re-layouts  1.29 us (3%)
    pallas_call x1, Pallas kernels, local(): pl.pallas_call(functools.partial(kernel, sizes), out_shape=(jax.ShapeDtyp...  44.2 us
    unnamed x1, local copies, waits for them, and re-layouts  1.29 us

profile of v3, /device:TPU:0, one launch (start us, length us, event | category | flops | bytes accessed | tf_op | source)
XLA Modules:
  0.0 47.9 jit_solution(15489619460087037766)
XLA Ops:
  0.6 44.2 %shard_map.104 = (f32[1,2,663]{2,1,0:T(2,128)}, f32[1,1]{1,0:T(1,128)}) custom-call(bf16[663,32,128]{2,1,0:T(8,128)(2,1)} %bitcast.3, s32[32,1326]{1,0:T(8,128)} %strengths.1, s32[32,1326]{1,0:T(8,128)} %live.1, f32[32,128]{1,0:T(8,128)} %pots.1, s32[32]{0:T(128)} %legal.1, s32[1,32]{1,0:T(1,128)} %bitcast.4, s32[16]{0:T(128)} %turn_legal.1, ...), custom_call_target="tpu_custom_call" | custom-call | tf_op jit(solution)/shard_map/pallas_call | solution.py:434
  44.8 1.3 %copy.13 = f32[1,2,663]{2,1,0:T(2,128)} copy(f32[1,2,663]{2,1,0:T(2,128)} %get-tuple-element.8) | data formatting | bytes 10608

commit v4 on v3

--- a/solution.py
+++ b/solution.py
@@ -51,7 +51,6 @@
     lines,
     row_s,
     row_live,
-    col_s,
     wide,
     small,
     pot_wide,
@@ -155,23 +154,16 @@
     for span in range(spans):
         peer_copy(span).start()
 
-    def turn_rows(tile, carry):
-        for side in range(2):
-            col_s[side * tiles + tile] = row_s[side, tile].T
-        return carry
-
-    lax.fori_loop(0, tiles, turn_rows, 0)
-
     table_copy.wait()
 
-    def compat_rows(tile, carry):
+    def wide_rows(tile, carry):
         at = pl.ds(pl.multiple_of(tile * LANE, LANE), LANE)
         for n in range(mine):
-            spread = jnp.broadcast_to(col_s[tile, :, n : n + 1], (LANE, LANE))
-            wide[n, at, :] = spread.astype(bf16)
+            block = jnp.broadcast_to(row_s[tile // tiles, lax.rem(tile, tiles), n : n + 1, :], (LANE, LANE))
+            wide[n, at, :] = block.astype(bf16).T
         return carry
 
-    lax.fori_loop(0, 2 * tiles, compat_rows, 0)
+    lax.fori_loop(0, 2 * tiles, wide_rows, 0)
 
     pot_block = jnp.concatenate(
         [pots[pl.ds(first_row, mine), :], jnp.zeros((LANE - mine, line_rows), f32)], axis=0
@@ -337,9 +329,10 @@
             lax.fori_loop(span * steps, (span + 1) * steps, functools.partial(one_step, b), 0)
             if b > 0 and span == 0:
                 sum_block(b - 1)
-            if b > 0 and span == spans - 1:
-                pass_block(b - 1)
-        river_copy(b).start()
+            if span == spans - 1:
+                river_copy(b).start()
+                if b > 0:
+                    pass_block(b - 1)
     sum_block(blocks - 1)
     pass_block(blocks - 1)
 
@@ -443,9 +436,8 @@
                 pltpu.VMEM((2, spans, tiles * LANE, TALL, line_rows), bf16),
                 [pltpu.VMEM((LANE * TALL, line_rows), f32) for _ in range(2)],
                 pltpu.VMEM((mine, 2 * tiles, line_rows, LANE), bf16),
-                pltpu.VMEM((2, tiles, LANE, LANE), f32),
                 pltpu.VMEM((2, tiles, mine, LANE), f32),
-                pltpu.VMEM((2 * tiles, LANE, LANE), f32),
+                pltpu.VMEM((2, tiles, mine, LANE), f32),
                 pltpu.VMEM((mine, 2 * tiles * LANE, LANE), bf16),
                 pltpu.VMEM((2 * tiles, 2 * tiles * LANE, LANE), jnp.int8),
                 pltpu.VMEM((mine, line_rows, LANE), f32),

time: 48.1 us -> 46.6 us (0.969)
  Pallas kernels: 44.2 us -> 42.7 us
    pallas_call x1, Pallas kernels: 44.2 us -> 42.7 us  [local(): pl.pallas_call(functools.partial(kernel, sizes), out_shape=(jax.ShapeDtyp...]
where the time goes in v4:
time: 46.6 us; the launch traced here: 46.4 us
  Pallas kernels  42.7 us (92%)
  between operations  2.4 us (5%)
  local copies, waits for them, and re-layouts  1.29 us (3%)
    pallas_call x1, Pallas kernels, local(): pl.pallas_call(functools.partial(kernel, sizes), out_shape=(jax.ShapeDtyp...  42.7 us
    unnamed x1, local copies, waits for them, and re-layouts  1.29 us

profile of v4, /device:TPU:0, one launch (start us, length us, event | category | flops | bytes accessed | tf_op | source)
XLA Modules:
  0.0 46.4 jit_solution(2339840286582364623)
XLA Ops:
  0.6 42.7 %shard_map.104 = (f32[1,2,663]{2,1,0:T(2,128)}, f32[1,1]{1,0:T(1,128)}) custom-call(bf16[663,32,128]{2,1,0:T(8,128)(2,1)} %bitcast.3, s32[32,1326]{1,0:T(8,128)} %strengths.1, s32[32,1326]{1,0:T(8,128)} %live.1, f32[32,128]{1,0:T(8,128)} %pots.1, s32[32]{0:T(128)} %legal.1, s32[1,32]{1,0:T(1,128)} %bitcast.4, s32[16]{0:T(128)} %turn_legal.1, ...), custom_call_target="tpu_custom_call" | custom-call | tf_op jit(solution)/shard_map/pallas_call | solution.py:427
  43.3 1.3 %copy.13 = f32[1,2,663]{2,1,0:T(2,128)} copy(f32[1,2,663]{2,1,0:T(2,128)} %get-tuple-element.8) | data formatting | bytes 10608

commit v5 on v4

--- a/solution.py
+++ b/solution.py
@@ -137,7 +137,8 @@
 
     for side in range(2):
         for span in range(spans):
-            raw[side, span, half:] = jnp.zeros((rows_k - half, TALL, LANE), bf16)
+            if used > half:
+                raw[side, span, half:used] = jnp.zeros((used - half, TALL, LANE), bf16)
 
     row_s[...] = jnp.zeros_like(row_s)
     row_live[...] = jnp.zeros_like(row_live)

time: 46.6 us -> 46.6 us (level)
  no operation moved by 1% of the time
where the time goes in v5:
time: 46.6 us; the launch traced here: 46.4 us
  Pallas kernels  42.7 us (92%)
  between operations  2.4 us (5%)
  local copies, waits for them, and re-layouts  1.29 us (3%)
    pallas_call x1, Pallas kernels, local(): pl.pallas_call(functools.partial(kernel, sizes), out_shape=(jax.ShapeDtyp...  42.7 us
    unnamed x1, local copies, waits for them, and re-layouts  1.29 us

profile of v5, /device:TPU:0, one launch (start us, length us, event | category | flops | bytes accessed | tf_op | source)
XLA Modules:
  0.0 46.4 jit_solution(16765742676700155471)
XLA Ops:
  0.6 42.7 %shard_map.104 = (f32[1,2,663]{2,1,0:T(2,128)}, f32[1,1]{1,0:T(1,128)}) custom-call(bf16[663,32,128]{2,1,0:T(8,128)(2,1)} %bitcast.3, s32[32,1326]{1,0:T(8,128)} %strengths.1, s32[32,1326]{1,0:T(8,128)} %live.1, f32[32,128]{1,0:T(8,128)} %pots.1, s32[32]{0:T(128)} %legal.1, s32[1,32]{1,0:T(1,128)} %bitcast.4, s32[16]{0:T(128)} %turn_legal.1, ...), custom_call_target="tpu_custom_call" | custom-call | tf_op jit(solution)/shard_map/pallas_call | solution.py:428
  43.3 1.3 %copy.13 = f32[1,2,663]{2,1,0:T(2,128)} copy(f32[1,2,663]{2,1,0:T(2,128)} %get-tuple-element.8) | data formatting | bytes 10608
